TPU v7x, 32 devices: a whole 2x2x4 slice. The times are simulated.
32 devices in a mesh: group: 4 (over y, x), fsdp: 2 (over core), tensor: 4 (over z).
Axes of the slice: x: 2, y: 2, z: 4, core: 2. Of those that a mesh axis runs over, the one named last changes fastest.
Arguments:
- patches: bfloat16 [4, 2, 8, 577, 1024], P('group', None, ('fsdp', 'tensor')), may hold values from -6 to 6
- output_grad: bfloat16 [4, 2, 8, 577, 1024], P('group', None, ('fsdp', 'tensor')), may hold values from -6 to 6
- live_counts: int32 [4, 2, 2], P('group'), may hold values from 1 to 4, as said below
- attn_master: float32 [4, 1024, 1024], P(None, 'fsdp', 'tensor')
- mlp_master: float32 [2, 1024, 4096], P(None, 'fsdp', 'tensor')
- vector_master: float32 [12, 1024], replicated
- attn_moments: float32 [4, 2, 4, 1024, 1024], P('group', None, None, 'fsdp', 'tensor'), as said below
- mlp_moments: float32 [4, 2, 2, 1024, 4096], P('group', None, None, 'fsdp', 'tensor'), as said below
- vector_moments: float32 [4, 2, 12, 1024], P('group'), as said below
- attn_outer: float32 [4, 1024, 1024], P(None, 'fsdp', 'tensor'), may hold values from -0.125 to 0.125
- mlp_outer: float32 [2, 1024, 4096], P(None, 'fsdp', 'tensor'), may hold values from -0.125 to 0.125
- vector_outer: float32 [12, 1024], replicated, may hold values from -0.625 to 0.625
Outputs:
- block_output: bfloat16 [4, 2, 8, 577, 1024], P('group', None, ('fsdp', 'tensor'))
- patches_grad: float32 [4, 2, 8, 577, 1024], P('group', None, ('fsdp', 'tensor'))
- attn_inner: float32 [4, 2, 4, 1024, 1024], P('group', None, None, 'fsdp', 'tensor')
- attn_state: float32 [3, 4, 1024, 1024], P(None, None, 'fsdp', 'tensor')
- attn_copy: bfloat16 [4, 1024, 1024], P(None, 'fsdp', 'tensor')
- mlp_inner: float32 [4, 2, 2, 1024, 4096], P('group', None, None, 'fsdp', 'tensor')
- mlp_state: float32 [3, 2, 1024, 4096], P(None, None, 'fsdp', 'tensor')
- mlp_copy: bfloat16 [2, 1024, 4096], P(None, 'fsdp', 'tensor')
- vector_inner: float32 [4, 2, 12, 1024], P('group')
- vector_state: float32 [3, 12, 1024], replicated
- vector_copy: bfloat16 [12, 1024], replicated
Inputs may be any that keep to these rules, and one draw needn't show every extreme that they name: live_counts[g, m, f] images are live, and they stand first, among the f-th block of 4 image slots of micro-batch m in group g; some entry equals 4. `attn_moments`: second moments are positive. `mlp_moments`: second moments are positive. `vector_moments`: second moments are positive.
All inputs are finite; a program needn't handle non-finite values.
Results may differ from a plain program's by a relative error of at most 0.012.
The roundings to bfloat16 on the way count: a program that leaves them out, or rounds other values in their place, can miss the bound.
Values may be sent and summed in bfloat16 or wider, within the bound.
A program may use at most 320 MiB of HBM per device.

v0:
```python
import jax
import jax.numpy as jnp
from jax import lax
from jax.sharding import PartitionSpec as P

HD = 64
STEP = 8
IMG_DEV = 4
EPSILON = 1e-06
INNER_RATE = 0.02
VECTOR_RATE = 0.2
WEIGHT_DECAY = 0.1
OUTER_RATE = 0.7
OUTER_MOMENTUM = 0.9


def normalize(source, gain_row, shift_row):
    centre = source - jnp.mean(source, axis=-1, keepdims=True)
    spread = jnp.mean(centre * centre, axis=-1, keepdims=True)
    return centre * lax.rsqrt(spread + EPSILON) * gain_row + shift_row


def gelu_exact(source):
    return jax.nn.gelu(source, approximate=False)


def gelu_slope(source):
    return (
        0.5 * (1.0 + lax.erf(source * 0.7071067811865476))
        + source * jnp.exp(-0.5 * source * source) * 0.3989422804014327
    )


def inner_adamw(master, gradient, moments, step_rate, decay_rate):
    first_moment = 0.9 * moments[0] + 0.1 * gradient
    second_moment = 0.95 * moments[1] + 0.05 * gradient * gradient
    step_ratio = (
        first_moment / (1.0 - 0.9**STEP) / (jnp.sqrt(second_moment / (1.0 - 0.95**STEP)) + 1e-08)
    )
    return (master - step_rate * (step_ratio + decay_rate * master), second_moment)


def outer_nesterov(master, outer_old, difference):
    momentum = OUTER_MOMENTUM * outer_old + difference
    updated = master - OUTER_RATE * (difference + OUTER_MOMENTUM * momentum)
    return (jnp.stack([difference, momentum, updated]), updated.astype(jnp.bfloat16))


def attend(queries, keys, values, score_scale):
    scores = (
        jnp.einsum("iqhe,ikhe->ihqk", queries, keys, preferred_element_type=jnp.float32)
        * score_scale
    )
    highest = jnp.max(scores, axis=-1, keepdims=True)
    exponent = jnp.exp(scores - highest)
    totals = jnp.sum(exponent, axis=-1, keepdims=True)
    return exponent / totals


def gather_weight(low):
    whole = lax.all_gather(low, "tensor", axis=2, tiled=True)
    return lax.all_gather(whole, "fsdp", axis=1, tiled=True)


def scatter_gradient(gradient):
    low = gradient.astype(jnp.bfloat16)
    half = lax.psum_scatter(low, "fsdp", scatter_dimension=1, tiled=True)
    return lax.psum_scatter(half, "tensor", scatter_dimension=2, tiled=True).astype(jnp.float32)


def local(
    patches,
    output_grad,
    live_counts,
    attn_master,
    mlp_master,
    vector_master,
    attn_moments,
    mlp_moments,
    vector_moments,
    attn_outer,
    mlp_outer,
    vector_outer,
):
    narrow = jnp.bfloat16
    single = jnp.float32
    tensor_index = lax.axis_index("tensor")
    fsdp_index = lax.axis_index("fsdp")
    micro_count, local_images, seq_len, width = patches.shape[1:]
    score_scale = HD ** (-0.5)
    attn_low = attn_master.astype(narrow)
    mlp_low = mlp_master.astype(narrow)
    tensor_size = lax.axis_size("tensor")
    image_slot = (fsdp_index * tensor_size + tensor_index) * local_images + jnp.arange(local_images)
    block = IMG_DEV
    counts = jnp.take(live_counts[0], image_slot // block, axis=1)
    alive = ((image_slot % block)[None, :] < counts).astype(single).reshape(-1, 1, 1)
    inputs = patches[0].astype(single).reshape(-1, seq_len, width)
    cotangent = output_grad[0].astype(single).reshape(-1, seq_len, width)
    image_count = inputs.shape[0]
    w_qkv = gather_weight(attn_low[:3])
    w_out = gather_weight(attn_low[3:])[0]
    w_in = gather_weight(mlp_low[:1])[0]
    w_down = gather_weight(mlp_low[1:])[0]
    vec = vector_master
    bias_hidden = vec[8:].reshape(-1)
    normed_one = normalize(inputs, vec[0], vec[1]).astype(narrow)
    projected = jnp.einsum("isd,jde->jise", normed_one, w_qkv, preferred_element_type=single)
    heads = width // HD
    shape_heads = (image_count, seq_len, heads, HD)
    queries = (projected[0] + vec[4]).astype(narrow).reshape(shape_heads)
    keys = projected[1].astype(narrow).reshape(shape_heads)
    values = (projected[2] + vec[5]).astype(narrow).reshape(shape_heads)
    probs = attend(queries, keys, values, score_scale)
    probs_low = probs.astype(narrow)
    attended = jnp.einsum("ihqk,ikhe->iqhe", probs_low, values, preferred_element_type=single)
    attended = attended.astype(narrow).reshape(image_count, seq_len, width)
    branch_one = jnp.einsum("ise,de->isd", attended, w_out, preferred_element_type=single)
    resid_one = inputs + branch_one + vec[6]
    normed_two = normalize(resid_one, vec[2], vec[3]).astype(narrow)
    pre_act = (
        jnp.einsum("isd,df->isf", normed_two, w_in, preferred_element_type=single) + bias_hidden
    )
    hidden = gelu_exact(pre_act).astype(narrow)
    grad_out = alive * cotangent
    grad_two = grad_out.astype(narrow)
    grad_down = jnp.einsum("isd,isf->df", grad_two, hidden, preferred_element_type=single)
    g_down = scatter_gradient(grad_down[None])
    branch_two = jnp.einsum("isf,df->isd", hidden, w_down, preferred_element_type=single)
    block_output = (alive * (resid_one + branch_two + vec[7])).astype(narrow)
    grad_hidden = jnp.einsum("isd,df->isf", grad_two, w_down, preferred_element_type=single)
    grad_pre = (grad_hidden * gelu_slope(pre_act)).astype(narrow)
    grad_in = jnp.einsum("isd,isf->df", normed_two, grad_pre, preferred_element_type=single)
    g_in = scatter_gradient(grad_in[None])
    grad_normed_two = jnp.einsum("isf,df->isd", grad_pre, w_in, preferred_element_type=single)
    unused_two, pull_two = jax.vjp(normalize, resid_one, vec[2], vec[3])
    back_resid, gain_two, shift_two = pull_two(grad_normed_two)
    grad_resid = grad_out + back_resid
    grad_one = grad_resid.astype(narrow)
    grad_wo = jnp.einsum("isd,ise->de", grad_one, attended, preferred_element_type=single)
    g_out = scatter_gradient(grad_wo[None])
    grad_attended = jnp.einsum("isd,de->ise", grad_one, w_out, preferred_element_type=single)
    grad_attended = grad_attended.astype(narrow).reshape(shape_heads)
    grad_probs = jnp.einsum("iqhe,ikhe->ihqk", grad_attended, values, preferred_element_type=single)
    grad_values = jnp.einsum(
        "ihqk,iqhe->ikhe", probs_low, grad_attended, preferred_element_type=single
    )
    weighted = jnp.sum(probs * grad_probs, axis=-1, keepdims=True)
    grad_scores = (probs * (grad_probs - weighted)).astype(narrow)
    grad_queries = (
        jnp.einsum("ihqk,ikhe->iqhe", grad_scores, keys, preferred_element_type=single)
        * score_scale
    )
    grad_keys = (
        jnp.einsum("ihqk,iqhe->ikhe", grad_scores, queries, preferred_element_type=single)
        * score_scale
    )
    stack = jnp.stack(
        [grad_queries.astype(narrow), grad_keys.astype(narrow), grad_values.astype(narrow)]
    )
    stack = stack.reshape(3, image_count, seq_len, width)
    grad_qkv = jnp.einsum("isd,jise->jde", normed_one, stack, preferred_element_type=single)
    g_qkv = scatter_gradient(grad_qkv)
    grad_normed_one = jnp.einsum("jise,jde->isd", stack, w_qkv, preferred_element_type=single)
    unused_one, pull_one = jax.vjp(normalize, inputs, vec[0], vec[1])
    back_inputs, gain_one, shift_one = pull_one(grad_normed_one)
    patches_grad = grad_resid + back_inputs
    vector_part = jnp.concatenate(
        [
            jnp.stack(
                [
                    gain_one,
                    shift_one,
                    gain_two,
                    shift_two,
                    jnp.sum(stack[0].astype(single), axis=(0, 1)),
                    jnp.sum(stack[2].astype(single), axis=(0, 1)),
                    jnp.sum(grad_resid, axis=(0, 1)),
                    jnp.sum(grad_out, axis=(0, 1)),
                ]
            ),
            jnp.sum(grad_pre.astype(single), axis=(0, 1)).reshape(-1, width),
        ]
    )
    vector_grad = lax.psum(vector_part, ("fsdp", "tensor"))
    attn_grad = jnp.concatenate([g_qkv, g_out])
    mlp_grad = jnp.concatenate([g_in, g_down])
    new_attn, second_attn = inner_adamw(
        attn_master, attn_grad, attn_moments[0], INNER_RATE, WEIGHT_DECAY
    )
    new_mlp, second_mlp = inner_adamw(
        mlp_master, mlp_grad, mlp_moments[0], INNER_RATE, WEIGHT_DECAY
    )
    new_vector, second_vector = inner_adamw(vec, vector_grad, vector_moments[0], VECTOR_RATE, 0.0)
    diff_attn, diff_mlp = lax.psum(
        ((attn_master - new_attn).astype(narrow), (mlp_master - new_mlp).astype(narrow)), "group"
    )
    diff_vector = lax.psum(vec - new_vector, "group")
    groups = lax.axis_size("group")
    attn_state, attn_copy = outer_nesterov(
        attn_master, attn_outer, diff_attn.astype(single) / groups
    )
    mlp_state, mlp_copy = outer_nesterov(mlp_master, mlp_outer, diff_mlp.astype(single) / groups)
    vector_state, vector_copy = outer_nesterov(vec, vector_outer, diff_vector / groups)
    shape_out = patches.shape
    return (
        block_output.reshape(shape_out),
        patches_grad.reshape(shape_out),
        jnp.stack([attn_grad, second_attn])[None],
        attn_state,
        attn_copy,
        jnp.stack([mlp_grad, second_mlp])[None],
        mlp_state,
        mlp_copy,
        jnp.stack([vector_grad, second_vector])[None],
        vector_state,
        vector_copy,
    )


def solution(mesh):
    placed = (
        P("group", None, ("fsdp", "tensor"), None, None),
        P("group", None, ("fsdp", "tensor"), None, None),
        P("group", None, None),
        P(None, "fsdp", "tensor"),
        P(None, "fsdp", "tensor"),
        P(),
        P("group", None, None, "fsdp", "tensor"),
        P("group", None, None, "fsdp", "tensor"),
        P("group", None, None, None),
        P(None, "fsdp", "tensor"),
        P(None, "fsdp", "tensor"),
        P(),
    )
    return jax.shard_map(
        local,
        mesh=mesh,
        in_specs=placed,
        out_specs=(
            P("group", None, ("fsdp", "tensor"), None, None),
            P("group", None, ("fsdp", "tensor"), None, None),
            P("group", None, None, "fsdp", "tensor"),
            P(None, None, "fsdp", "tensor"),
            P(None, "fsdp", "tensor"),
            P("group", None, None, "fsdp", "tensor"),
            P(None, None, "fsdp", "tensor"),
            P(None, "fsdp", "tensor"),
            P("group", None, None, None),
            P(),
            P(),
        ),
        check_vma=False,
    )
```

profile of v0, /device:TPU:0, one launch (start us, length us, event | category | flops | bytes accessed | tf_op | source)
XLA Modules:
  0.0 1130.8 jit_solution(4393395515950830453)
XLA Ops:
  15.4 60.9 %all-gather.9.cloned.1.call-done = bf16[3,512,1024]{2,1,0:T(8,128)(2,1)} async-done(((bf16[3,512,256]{2,1,0:T(8,128)(2,1)}), bf16[3,512,1024]{2,1,0:T(8,128)(2,1)}) %all-gather.9.cloned.1.call-update) | async-done | bytes 3145744 | tf_op jit(solution)/shard_map/all_gather | solution.py:61
  76.4 30.5 %all-gather.13.cloned.1.call-done = bf16[1,512,1024]{2,1,0:T(8,128)(2,1)} async-done(((bf16[1,512,256]{2,1,0:T(8,128)(2,1)}), bf16[1,512,1024]{2,1,0:T(8,128)(2,1)}) %all-gather.13.cloned.1.call-update) | async-done | bytes 1048592 | tf_op jit(solution)/shard_map/all_gather | solution.py:61
  106.9 81.2 %all-gather.17.cloned.1.call-done = bf16[1,512,4096]{2,1,0:T(8,128)(2,1)} async-done(((bf16[1,512,1024]{2,1,0:T(8,128)(2,1)}), bf16[1,512,4096]{2,1,0:T(8,128)(2,1)}) %all-gather.17.cloned.1.call-update) | async-done | bytes 4194320 | tf_op jit(solution)/shard_map/all_gather | solution.py:61
  190.9 78.5 %all-gather.21.cloned.1.call-done = bf16[1,512,4096]{2,1,0:T(8,128)(2,1)} async-done(((bf16[1,512,1024]{2,1,0:T(8,128)(2,1)}), bf16[1,512,4096]{2,1,0:T(8,128)(2,1)}) %all-gather.21.cloned.1.call-update) | async-done | bytes 4194320 | tf_op jit(solution)/shard_map/all_gather | solution.py:61
  270.0 16.1 %all-gather.11.cloned.1.call-done = bf16[3,1024,1024]{2,1,0:T(8,128)(2,1)} async-done(((bf16[3,512,1024]{2,1,0:T(8,128)(2,1)}), bf16[3,1024,1024]{2,1,0:T(8,128)(2,1)}) %all-gather.11.cloned.1.call-update) | async-done | bytes 6291472 | tf_op jit(solution)/shard_map/all_gather | solution.py:62
  332.0 23.1 %fusion.156 = (f32[2,16,577]{2,1,0:T(8,128)S(1)}, f32[2,16,577,577]{2,3,1,0:T(8,128)}) fusion(bf16[2,577,16,64]{1,3,2,0:T(8,128)(2,1)} %bitcast.296, f32[2,577,16,64]{1,3,2,0:T(8,128)} %bitcast.293, f32[16,64]{1,0:T(8,128)S(1)} %add.245), kind=kOutput, calls=%fused_computation.230 | convolution fusion | flops 1398002304 | bytes 49783040 | tf_op jit(solution)/shard_map/sub | solution.py:55
  355.1 19.5 %fusion.99 = bf16[2,16,64,577]{3,2,1,0:T(8,128)(2,1)} fusion(f32[2,577,16,64]{1,3,2,0:T(8,128)} %bitcast.299, f32[16,64]{1,0:T(8,128)S(1)} %add.242, f32[2,16,577,577]{2,3,1,0:T(8,128)} %get-tuple-element.104, f32[2,16,577]{2,1,0:T(8,128)S(1)} %get-tuple-element.103), kind=kOutput, calls=%fused_computation.157 | convolution fusion | flops 1388529664 | bytes 49783040 | tf_op jit(solution)/shard_map/ihqk,ikhe->iqhe/dot_general | solution.py:116
  383.7 27.9 %fusion.61 = (u8[577,4096]{1,0:T(8,128)(4,1)}, u8[577,4096]{1,0:T(8,128)(4,1)}, f32[2,577,4096]{2,1,0:T(8,128)}) fusion(f32[4096]{0:T(1024)S(1)} %bitcast.306, bf16[1,1024,4096]{2,1,0:T(8,128)(2,1)} %all-gather.19.cloned.1.call-done, f32[2,577,1024]{2,1,0:T(8,128)} %copy-done, f32[1024]{0:T(1024)S(1)} %bitcast.325, f32[1024]{0:T(1024)S(1)} %bitcast.314, ...), kind=kOutput, calls=%fused_computation.108 | convolution fusion | flops 9747810304 | bytes 36783120 | tf_op jit(solution)/shard_map/isd,df->isf/dot_general | solution.py:122
  411.6 23.1 %convert_reduce_fusion = (f32[4096]{0:T(1024)}, bf16[2,577,4096]{2,1,0:T(8,128)(2,1)}) fusion(f32[2,577,4096]{2,1,0:T(8,128)} %get-tuple-element.107, f32[4096]{0:T(1024)S(1)} %bitcast.307, bf16[1,1024,4096]{2,1,0:T(8,128)(2,1)} %all-gather.23.cloned.1.call-done, f32[2]{0:T(128)S(1)} %fusion.136, bf16[1,2,1,577,1024]{4,1,3,2,0:T(2,128)(2,1)S(1)} %copy-done.17), kind=kOutput, calls=%fused_computation.24 | convolution fusion | flops 9745442816 | bytes 39145480 | tf_op jit(solution)/shard_map/isd,df->isf/dot_general | solution.py:131
  434.7 17.4 %fusion.146 = (f32[1024]{0:T(1024)}, f32[2,577]{1,0:T(2,128)S(1)}, f32[2,577,1024]{2,1,0:T(8,128)}) fusion(f32[1024]{0:T(1024)S(1)} %bitcast.315, f32[2,577,1024]{2,1,0:T(8,128)S(1)} %bitcast.290, f32[2,577]{1,0:T(2,128)S(1)} %broadcast_multiply_fusion, bf16[2,577,4096]{2,1,0:T(8,128)(2,1)} %get-tuple-element.117, ...), kind=kOutput, calls=%fused_computation.221 | convolution fusion | flops 9686360064 | bytes 27313168 | tf_op jit(solution)/shard_map/isf,df->isd/dot_general | solution.py:135
  475.9 19.5 %convert_reduce_fusion.2 = (f32[16,64]{1,0:T(8,128)}, bf16[2,16,64,577]{3,2,1,0:T(8,128)(2,1)}) fusion(bf16[2,577,16,64]{1,3,2,0:T(8,128)(2,1)S(1)} %bitcast.302, f32[2,16,577,577]{2,3,1,0:T(8,128)} %get-tuple-element.104, f32[2,16,577]{2,1,0:T(8,128)S(1)} %get-tuple-element.103), kind=kOutput, calls=%fused_computation.81 | convolution fusion | flops 1388528640 | bytes 47419648 | tf_op jit(solution)/shard_map/ihqk,iqhe->ikhe/dot_general | solution.py:145
  495.3 39.2 %multiply_reduce_fusion = (f32[2,16,577]{2,1,0:T(8,128)S(1)}, f32[2,16,577,577]{2,3,1,0:T(8,128)}) fusion(f32[2,16,577,577]{2,3,1,0:T(8,128)} %get-tuple-element.104, f32[2,16,577]{2,1,0:T(8,128)S(1)} %get-tuple-element.103, bf16[2,577,16,64]{1,3,2,0:T(8,128)(2,1)S(1)} %bitcast.303, f32[2,577,16,64]{1,3,2,0:T(8,128)} %bitcast.300, f32[16,64]{1,0:T(8,128)S(1)} %copy-done.56), kind=kOutput, calls=%fused_computation.2 | convolution fusion | flops 1397983232 | bytes 92471808 | tf_op jit(solution)/shard_map/iqhe,ikhe->ihqk/dot_general | solution.py:144
  534.6 39.2 %multiply_convert_fusion = bf16[2,16,577,577]{2,3,1,0:T(8,128)(2,1)} fusion(f32[2,16,577,577]{2,3,1,0:T(8,128)} %get-tuple-element.110, f32[2,16,577]{2,1,0:T(8,128)S(1)} %get-tuple-element.109, f32[2,16,577,577]{2,3,1,0:T(8,128)} %get-tuple-element.104, f32[2,16,577]{2,1,0:T(8,128)S(1)} %get-tuple-element.103), kind=kLoop, calls=%fused_computation.1 | loop fusion | flops 42614912 | bytes 106684992 | tf_op jit(solution)/shard_map/convert_element_type | solution.py:149
  626.3 18.6 %fusion.31 = bf16[1,1024,4096]{2,1,0:T(8,128)(2,1)} fusion(bf16[2,577,4096]{2,1,0:T(8,128)(2,1)} %get-tuple-element.117, f32[2,577,1024]{2,1,0:T(8,128)} %copy-done, f32[1024]{0:T(1024)S(1)} %bitcast.326, f32[1024]{0:T(1024)S(1)} %bitcast.318, f32[2,577]{1,0:T(2,128)S(1)} %copy-done.41, f32[2,577]{1,0:T(2,128)S(1)} %copy-done.29), kind=kOutput, calls=%fused_computation.57 | convolution fusion | flops 9690556416 | bytes 22586384 | tf_op jit(solution)/shard_map/isd,isf->df/dot_general | solution.py:133
  645.6 46.9 %fusion.7 = bf16[2,577,4096]{2,1,0:T(8,128)(2,1)S(1)} fusion(f32[2,577,4096]{2,1,0:T(8,128)} %get-tuple-element.107, f32[4096]{0:T(1024)S(1)} %bitcast.308, u8[577,4096]{1,0:T(8,128)(4,1)} %get-tuple-element.45, u8[577,4096]{1,0:T(8,128)(4,1)} %get-tuple-element.44), kind=kLoop, calls=%fused_computation.12 | loop fusion | flops 335601664 | bytes 33103872 | tf_op jit(solution)/shard_map/convert_element_type | solution.py:124
  696.3 15.0 %fusion.32 = bf16[1,1024,4096]{2,1,0:T(8,128)(2,1)} fusion(bf16[2,577,4096]{2,1,0:T(8,128)(2,1)S(1)} %fusion.7, f32[2]{0:T(128)S(1)} %copy-done.65, bf16[1,2,1,577,1024]{4,1,3,2,0:T(2,128)(2,1)S(1)} %copy-done.18), kind=kOutput, calls=%fused_computation.58 | convolution fusion | flops 9688193024 | bytes 20205576 | tf_op jit(solution)/shard_map/isd,isf->df/dot_general | solution.py:127
  713.3 16.1 %reduce-scatter.21.cloned.1.call-done = bf16[1,512,4096]{2,1,0:T(8,128)(2,1)} async-done(((bf16[1,1024,4096]{2,1,0:T(8,128)(2,1)}), bf16[1,512,4096]{2,1,0:T(8,128)(2,1)}) %reduce-scatter.21.cloned.1.call-update) | async-done | bytes 4194320 | tf_op jit(solution)/shard_map/reduce_scatter | solution.py:67
  746.6 15.2 %bitcast_reduce_fusion = (f32[1024]{0:T(1024)}, f32[2,577]{1,0:T(2,128)S(1)}, f32[2,577,1024,1]{2,1,3,0:T(8,128)}) fusion(f32[1024]{0:T(1024)S(1)} %bitcast.311, f32[2,577]{1,0:T(2,128)S(1)} %copy-done.27, bf16[1,2,1,577,1024]{4,1,3,2,0:T(2,128)(2,1)S(1)} %copy-done.2, bf16[3,1024,1024]{2,1,0:T(8,128)(2,1)} %all-gather.11.cloned.1.call-done, ...), kind=kOutput, calls=%fused_computation.99 | convolution fusion | flops 7274518528 | bytes 20489232 | tf_op jit(solution)/shard_map/jise,jde->isd/dot_general | solution.py:164
  761.8 16.4 %fusion.76 = bf16[1,2,1,577,1024]{4,3,1,2,0:T(8,128)(2,1)} fusion(f32[2,577,1024]{2,1,0:T(8,128)S(1)} %bitcast.292, f32[1024]{0:T(1024)S(1)} %bitcast.324, f32[2]{0:T(128)S(1)} %copy-done.65, bf16[2,577,4096]{2,1,0:T(8,128)(2,1)} %copy-done.13, bf16[1,1024,4096]{2,1,0:T(8,128)(2,1)} %all-gather.23.cloned.1.call-done), kind=kOutput, calls=%fused_computation.133 | convolution fusion | flops 9685180416 | bytes 24936456 | tf_op jit(solution)/shard_map/isf,df->isd/dot_general | solution.py:129
  779.2 42.1 %reduce-scatter.11.cloned.1.call-done = bf16[3,512,256]{1,2,0:T(8,128)(2,1)} async-done(((bf16[3,512,1024]{1,2,0:T(8,128)(2,1)}), bf16[3,512,256]{1,2,0:T(8,128)(2,1)}) %reduce-scatter.11.cloned.1.call-update) | async-done | bytes 786448 | tf_op jit(solution)/shard_map/reduce_scatter | solution.py:68
  829.7 70.7 %reduce-scatter.19.cloned.1.call-done = bf16[1,512,1024]{2,1,0:T(8,128)(2,1)} async-done(((bf16[1,512,4096]{2,1,0:T(8,128)(2,1)}), bf16[1,512,1024]{2,1,0:T(8,128)(2,1)}) %reduce-scatter.19.cloned.1.call-update) | async-done | bytes 1048592 | tf_op jit(solution)/shard_map/reduce_scatter | solution.py:68
  904.3 75.6 %reduce-scatter.23.cloned.1.call-done = bf16[1,512,1024]{2,1,0:T(8,128)(2,1)} async-done(((bf16[1,512,4096]{2,1,0:T(8,128)(2,1)}), bf16[1,512,1024]{2,1,0:T(8,128)(2,1)}) %reduce-scatter.23.cloned.1.call-update) | async-done | bytes 1048592 | tf_op jit(solution)/shard_map/reduce_scatter | solution.py:68
  1017.4 28.7 %psum.30 = f32[12,1024]{1,0:T(8,128)S(1)} all-reduce(f32[12,1024]{1,0:T(8,128)S(1)} %concatenate.56), channel_id=1, replica_groups=mesh['group'=4,'fsdp'=2,'tensor'=4] {'fsdp','tensor'}, use_global_device_ids=true, to_apply=%region_30.31 | all-reduce | flops 12288 | bytes 98304 | tf_op jit(solution)/shard_map/psum | solution.py:185
  1047.0 17.7 %psum.31 = f32[12,1024]{1,0:T(8,128)S(1)} all-reduce(f32[12,1024]{1,0:T(8,128)S(1)} %get-tuple-element.90), channel_id=1, replica_groups=mesh['group'=4,'fsdp'=2,'tensor'=4] {'group'}, use_global_device_ids=true, to_apply=%region_31.32 | all-reduce | flops 12288 | bytes 98304 | tf_op jit(solution)/shard_map/psum | solution.py:198
  (266 shorter events, 276.2 us)
Async XLA Ops:
  7.2 69.1 %all-gather.9.cloned.1.call-start = ((), (), s32[]{:S(2)}) async-start(), calls=%async_computation.8 | async-start | bytes 3932160 | tf_op jit(solution)/shard_map/all_gather | solution.py:61
  9.9 97.0 %all-gather.13.cloned.1.call-start = ((), (), s32[]{:S(2)}) async-start(), calls=%async_computation.10 | async-start | bytes 1310720 | tf_op jit(solution)/shard_map/all_gather | solution.py:61
  10.7 177.4 %all-gather.17.cloned.1.call-start = ((), (), s32[]{:S(2)}) async-start(), calls=%async_computation.12 | async-start | bytes 5242880 | tf_op jit(solution)/shard_map/all_gather | solution.py:61
  14.8 254.7 %all-gather.21.cloned.1.call-start = ((), (), s32[]{:S(2)}) async-start(), calls=%async_computation.14 | async-start | bytes 5242880 | tf_op jit(solution)/shard_map/all_gather | solution.py:61
  14.8 174.2 %copy-start.66 = (s32[1,2,2]{2,1,0:T(2,128)S(1)}, s32[1,2,2]{2,1,0:T(2,128)}, u32[]{:S(2)}) copy-start(s32[1,2,2]{2,1,0:T(2,128)} %param.14) | copy-start | bytes 52
  14.8 174.4 %copy-start.1 = (bf16[1,2,1,577,1024]{4,1,3,2,0:T(2,128)(2,1)S(1)}, bf16[1,2,1,577,1024]{4,1,3,2,0:T(2,128)(2,1)}, u32[]{:S(2)}) copy-start(bf16[1,2,1,577,1024]{4,1,3,2,0:T(2,128)(2,1)} %param.12) | copy-start | bytes 7090180
  15.3 270.8 %all-gather.11.cloned.1.call-start = ((), (), s32[]{:S(2)}) async-start(), calls=%async_computation.9 | async-start | bytes 9437184 | tf_op jit(solution)/shard_map/all_gather | solution.py:62
  76.3 298.3 %all-gather.15.cloned.1.call-start = ((), (), s32[]{:S(2)}) async-start(), calls=%async_computation.11 | async-start | bytes 3145728 | tf_op jit(solution)/shard_map/all_gather | solution.py:62
  106.9 276.8 %all-gather.19.cloned.1.call-start = ((), (), s32[]{:S(2)}) async-start(), calls=%async_computation.13 | async-start | bytes 12582912 | tf_op jit(solution)/shard_map/all_gather | solution.py:62
  188.1 223.4 %all-gather.23.cloned.1.call-start = ((), (), s32[]{:S(2)}) async-start(), calls=%async_computation.15 | async-start | bytes 12582912 | tf_op jit(solution)/shard_map/all_gather | solution.py:62
  188.2 223.3 %copy-start.30 = (f32[1,8,4,128]{3,1,2,0:T(8,128)}, f32[1,8,4,128]{3,1,2,0:T(8,128)S(1)}, u32[]{:S(2)}) copy-start(f32[1,8,4,128]{3,1,2,0:T(8,128)S(1)} %copy.159) | copy-start | bytes 49156
  188.9 194.8 %copy-start.59 = (f32[1,1024]{1,0:T(1,128)}, f32[1,1024]{1,0:T(1,128)S(1)}, u32[]{:S(2)}) copy-start(f32[1,1024]{1,0:T(1,128)S(1)} %get-tuple-element.97) | copy-start | bytes 12292
  188.9 267.9 %copy-start.44 = (f32[1,1024]{1,0:T(1,128)}, f32[1,1024]{1,0:T(1,128)S(1)}, u32[]{:S(2)}) copy-start(f32[1,1024]{1,0:T(1,128)S(1)} %get-tuple-element.95) | copy-start | bytes 12292
  189.2 267.6 %copy-start.64 = (f32[2]{0:T(128)}, f32[2]{0:T(128)S(1)}, u32[]{:S(2)}) copy-start(f32[2]{0:T(128)S(1)} %fusion.136) | copy-start | bytes 28
  269.5 442.0 %reduce-scatter.13.cloned.1.call-start = ((), (), s32[]{:S(2)}) async-start(), calls=%async_computation.18 | async-start | bytes 3145728 | tf_op jit(solution)/shard_map/reduce_scatter | solution.py:67
  534.5 177.6 %reduce-scatter.9.cloned.1.call-start = ((), (), s32[]{:S(2)}) async-start(), calls=%async_computation.16 | async-start | bytes 9437184 | tf_op jit(solution)/shard_map/reduce_scatter | solution.py:67
  625.6 87.2 %reduce-scatter.17.cloned.1.call-start = ((), (), s32[]{:S(2)}) async-start(), calls=%async_computation.20 | async-start | bytes 12582912 | tf_op jit(solution)/shard_map/reduce_scatter | solution.py:67
  644.9 84.5 %reduce-scatter.21.cloned.1.call-start = ((), (), s32[]{:S(2)}) async-start(), calls=%async_computation.22 | async-start | bytes 12582912 | tf_op jit(solution)/shard_map/reduce_scatter | solution.py:67
  711.4 66.8 %reduce-scatter.15.cloned.1.call-start = ((), (), s32[]{:S(2)}) async-start(), calls=%async_computation.19 | async-start | bytes 1310720 | tf_op jit(solution)/shard_map/reduce_scatter | solution.py:68
  712.1 109.3 %reduce-scatter.11.cloned.1.call-start = ((), (), s32[]{:S(2)}) async-start(), calls=%async_computation.17 | async-start | bytes 3932160 | tf_op jit(solution)/shard_map/reduce_scatter | solution.py:68
  712.7 187.7 %reduce-scatter.19.cloned.1.call-start = ((), (), s32[]{:S(2)}) async-start(), calls=%async_computation.21 | async-start | bytes 5242880 | tf_op jit(solution)/shard_map/reduce_scatter | solution.py:68
  713.3 266.6 %reduce-scatter.23.cloned.1.call-start = ((), (), s32[]{:S(2)}) async-start(), calls=%async_computation.23 | async-start | bytes 5242880 | tf_op jit(solution)/shard_map/reduce_scatter | solution.py:68
  729.5 355.1 %all-reduce.3.cloned.1.call-start = ((), (), s32[]{:S(2)}) async-start(), calls=%async_computation.24 | async-start | bytes 6291456 | tf_op jit(solution)/shard_map/psum | solution.py:195
  761.8 229.1 %copy-start.36 = (f32[2,577]{1,0:T(2,128)}, f32[2,577]{1,0:T(2,128)S(1)}, u32[]{:S(2)}) copy-start(f32[2,577]{1,0:T(2,128)S(1)} %multiply_multiply_fusion.11) | copy-start | bytes 13852
  (66 other events, 1921.4 us)
Sparse Core Ops, SparseCore 0:
  10.1 66.1 all-gather.8
  78.4 28.3 all-gather.12
  109.0 79.0 all-gather.16
  190.1 79.2 all-gather.20
  270.8 15.2 all-gather.10
  287.5 11.7 all-gather.14
  300.9 21.0 all-gather.18
  323.5 21.0 all-gather.22
  534.6 10.7 reduce-scatter.12
  625.7 15.6 reduce-scatter.8
  645.0 17.9 reduce-scatter.16
  711.5 17.9 reduce-scatter.20
  731.7 28.3 reduce-scatter.14
  762.4 58.8 reduce-scatter.10
  823.6 76.7 reduce-scatter.18
  902.6 77.2 reduce-scatter.22
  991.0 88.6 all-reduce.2
where the time goes:
time: 1130 us
  waiting for transfers between devices  474 us (42%)
  matrix products  303 us (27%)
  other arithmetic  182 us (16%)
  local copies, waits for them, and re-layouts  108 us (10%)
  blocking collectives  46.5 us (4%)
  between operations  15.3 us (1%)
    all_gather x4, waiting for transfers between devices, gather_weight(): whole = lax.all_gather(low, 'tensor', axis=2, tiled=True)  251 us
    reduce_scatter x4, waiting for transfers between devices, scatter_gradient(): lax.psum_scatter(half, 'tensor', scatter_dimension=2, tiled=True)  188 us
    unnamed x157, local copies, waits for them, and re-layouts  53.4 us
    convert_element_type x1, other arithmetic, local(): hidden = gelu_exact(pre_act).astype(narrow)  46.9 us
    convert_element_type x1, other arithmetic, local(): grad_scores = (probs * (grad_probs - weighted)).astype(narrow)  39.2 us
    dot_general x1, matrix products, local(): jnp.einsum('iqhe,ikhe->ihqk', grad_attended, values, preferred_element_ty...  39.2 us
    psum x1, blocking collectives, local(): vector_grad = lax.psum(vector_part, ('fsdp', 'tensor'))  28.7 us
    dot_general x1, matrix products, local(): jnp.einsum('isd,df->isf', normed_two, w_in, preferred_element_type=single)  27.9 us
  transfers between devices with their start and end apart: 17, of which 9 were waited for; matrix products, arithmetic and copies ran while one was open for 36% of the time, Pallas kernels for 0%

commit v1 on v0

--- a/solution.py
+++ b/solution.py
@@ -58,7 +58,16 @@
 
 
 def gather_weight(low):
-    whole = lax.all_gather(low, "tensor", axis=2, tiled=True)
+    value = low
+    ways, here, step = (lax.axis_size("tensor"), lax.axis_index("tensor"), value.shape[2])
+    shape = [n * ways if d == 2 else n for d, n in enumerate(value.shape)]
+    full = lax.dynamic_update_slice_in_dim(
+        jnp.zeros(shape, value.dtype), value, here * step, axis=2
+    )
+    for far in range(1, ways):
+        value = lax.ppermute(value, "tensor", [(d, (d + 1) % ways) for d in range(ways)])
+        full = lax.dynamic_update_slice_in_dim(full, value, (here - far) % ways * step, axis=2)
+    whole = full
     return lax.all_gather(whole, "fsdp", axis=1, tiled=True)
 
 

time: 1130 us -> 1090 us (0.965)
  waiting for transfers between devices: 474 us -> 399 us
  local copies, waits for them, and re-layouts: 108 us -> 132 us
    all_gather x4 -> x0, waiting for transfers between devices: 251 us -> none  [gather_weight(): whole = lax.all_gather(low, 'tensor', axis=2, tiled=True)]
    ppermute x0 -> x12, waiting for transfers between devices: none -> 196 us  [gather_weight(): lax.ppermute(value, 'tensor', [(d, (d + 1) % ways) for d in range(ways)])]
    all_gather x4, waiting for transfers between devices: 16.2 us -> 0.06 us  [gather_weight(): return lax.all_gather(whole, 'fsdp', axis=1, tiled=True)]
    dynamic_update_slice x0 -> x13, local copies, waits for them, and re-layouts: none -> 14.9 us  [the longest x12 13.9 us: gather_weight(): lax.dynamic_update_slice_in_dim(full, value, (here - far) % ways * step,...]
    unnamed x157 -> x167, local copies, waits for them, and re-layouts: 53.4 us -> 56.9 us
  transfers between devices with their start and end apart: 17 -> 25, of which waited for: 9 -> 15; matrix products, arithmetic and copies ran while one was open for 36% -> 39% of each run, Pallas kernels for 0% -> 0%
where the time goes in v1:
time: 1090 us; the launch traced here: 1080 us
  waiting for transfers between devices  399 us (37%)
  matrix products  303 us (28%)
  other arithmetic  183 us (17%)
  local copies, waits for them, and re-layouts  132 us (12%)
  blocking collectives  46.5 us (4%)
  between operations  15.4 us (1%)
    ppermute x12, waiting for transfers between devices, gather_weight(): lax.ppermute(value, 'tensor', [(d, (d + 1) % ways) for d in range(ways)])  196 us
    reduce_scatter x4, waiting for transfers between devices, scatter_gradient(): lax.psum_scatter(half, 'tensor', scatter_dimension=2, tiled=True)  189 us
    unnamed x167, local copies, waits for them, and re-layouts  56.9 us
    convert_element_type x1, other arithmetic, local(): hidden = gelu_exact(pre_act).astype(narrow)  46.9 us
    convert_element_type x1, other arithmetic, local(): grad_scores = (probs * (grad_probs - weighted)).astype(narrow)  39.1 us
    dot_general x1, matrix products, local(): jnp.einsum('iqhe,ikhe->ihqk', grad_attended, values, preferred_element_ty...  38.9 us
    psum x1, blocking collectives, local(): vector_grad = lax.psum(vector_part, ('fsdp', 'tensor'))  28.7 us
    dot_general x1, matrix products, local(): jnp.einsum('isd,df->isf', normed_two, w_in, preferred_element_type=single)  27.9 us
  transfers between devices with their start and end apart: 25, of which 15 were waited for; matrix products, arithmetic and copies ran while one was open for 39% of the time, Pallas kernels for 0%

profile of v1, /device:TPU:0, one launch (start us, length us, event | category | flops | bytes accessed | tf_op | source)
XLA Modules:
  0.0 1082.9 jit_solution(4523581932190049557)
XLA Ops:
  14.7 19.6 %collective-permute-done = bf16[3,512,256]{2,1,0:T(8,128)(2,1)S(1)} collective-permute-done((bf16[3,512,256]{2,1,0:T(8,128)(2,1)S(1)}, bf16[3,512,256]{2,1,0:T(8,128)(2,1)S(1)}, u32[]{:S(2)}, u32[]{:S(2)}) %collective-permute-start) | collective-permute-done | bytes 786464 | tf_op jit(solution)/shard_map/ppermute | solution.py:68
  35.1 20.6 %collective-permute-done.1 = bf16[3,512,256]{2,1,0:T(8,128)(2,1)} collective-permute-done((bf16[3,512,256]{2,1,0:T(8,128)(2,1)S(1)}, bf16[3,512,256]{2,1,0:T(8,128)(2,1)}, u32[]{:S(2)}, u32[]{:S(2)}) %collective-permute-start.1) | collective-permute-done | bytes 786464 | tf_op jit(solution)/shard_map/ppermute | solution.py:68
  58.2 17.4 %collective-permute-done.2 = bf16[3,512,256]{2,1,0:T(8,128)(2,1)} collective-permute-done((bf16[3,512,256]{2,1,0:T(8,128)(2,1)}, bf16[3,512,256]{2,1,0:T(8,128)(2,1)}, u32[]{:S(2)}, u32[]{:S(2)}) %collective-permute-start.2) | collective-permute-done | bytes 786464 | tf_op jit(solution)/shard_map/ppermute | solution.py:68
  86.8 28.6 %collective-permute-done.3 = bf16[1,512,256]{2,1,0:T(8,128)(2,1)S(1)} collective-permute-done((bf16[1,512,256]{2,1,0:T(8,128)(2,1)S(1)}, bf16[1,512,256]{2,1,0:T(8,128)(2,1)S(1)}, u32[]{:S(2)}, u32[]{:S(2)}) %collective-permute-start.3) | collective-permute-done | bytes 262176 | tf_op jit(solution)/shard_map/ppermute | solution.py:68
  135.8 16.6 %collective-permute-done.7 = bf16[1,512,1024]{2,1,0:T(8,128)(2,1)} collective-permute-done((bf16[1,512,1024]{2,1,0:T(8,128)(2,1)}, bf16[1,512,1024]{2,1,0:T(8,128)(2,1)}, u32[]{:S(2)}, u32[]{:S(2)}) %collective-permute-start.7) | collective-permute-done | bytes 1048608 | tf_op jit(solution)/shard_map/ppermute | solution.py:68
  157.1 17.4 %collective-permute-done.8 = bf16[1,512,1024]{2,1,0:T(8,128)(2,1)S(1)} collective-permute-done((bf16[1,512,1024]{2,1,0:T(8,128)(2,1)}, bf16[1,512,1024]{2,1,0:T(8,128)(2,1)S(1)}, u32[]{:S(2)}, u32[]{:S(2)}) %collective-permute-start.8) | collective-permute-done | bytes 1048608 | tf_op jit(solution)/shard_map/ppermute | solution.py:68
  175.8 23.5 %collective-permute-done.9 = bf16[1,512,1024]{2,1,0:T(8,128)(2,1)S(1)} collective-permute-done((bf16[1,512,1024]{2,1,0:T(8,128)(2,1)}, bf16[1,512,1024]{2,1,0:T(8,128)(2,1)S(1)}, u32[]{:S(2)}, u32[]{:S(2)}) %collective-permute-start.9) | collective-permute-done | bytes 1048608 | tf_op jit(solution)/shard_map/ppermute | solution.py:68
  201.0 21.4 %collective-permute-done.10 = bf16[1,512,1024]{2,1,0:T(8,128)(2,1)} collective-permute-done((bf16[1,512,1024]{2,1,0:T(8,128)(2,1)S(1)}, bf16[1,512,1024]{2,1,0:T(8,128)(2,1)}, u32[]{:S(2)}, u32[]{:S(2)}) %collective-permute-start.10) | collective-permute-done | bytes 1048608 | tf_op jit(solution)/shard_map/ppermute | solution.py:68
  287.8 22.3 %fusion.156 = (f32[2,16,577]{2,1,0:T(8,128)S(1)}, f32[2,16,577,577]{2,3,1,0:T(8,128)}) fusion(bf16[2,577,16,64]{1,3,2,0:T(8,128)(2,1)} %bitcast.299, f32[2,577,16,64]{1,3,2,0:T(8,128)} %bitcast.296, f32[16,64]{1,0:T(8,128)S(1)} %add.306), kind=kOutput, calls=%fused_computation.250 | convolution fusion | flops 1398002304 | bytes 49783040 | tf_op jit(solution)/shard_map/sub | solution.py:55
  310.1 19.5 %fusion.96 = bf16[2,16,64,577]{3,2,1,0:T(8,128)(2,1)} fusion(f32[2,577,16,64]{1,3,2,0:T(8,128)} %bitcast.302, f32[16,64]{1,0:T(8,128)S(1)} %add.303, f32[2,16,577,577]{2,3,1,0:T(8,128)} %get-tuple-element.109, f32[2,16,577]{2,1,0:T(8,128)S(1)} %get-tuple-element.108), kind=kOutput, calls=%fused_computation.157 | convolution fusion | flops 1388529664 | bytes 49783040 | tf_op jit(solution)/shard_map/ihqk,ikhe->iqhe/dot_general | solution.py:125
  338.7 27.9 %fusion.57 = (u8[577,4096]{1,0:T(8,128)(4,1)}, u8[577,4096]{1,0:T(8,128)(4,1)}, f32[2,577,4096]{2,1,0:T(8,128)}) fusion(f32[4096]{0:T(1024)S(1)} %bitcast.309, bf16[1,1024,4096]{2,1,0:T(8,128)(2,1)} %all-gather.9.cloned.1.call-done, f32[2,577,1024]{2,1,0:T(8,128)} %copy-done, f32[1024]{0:T(1024)S(1)} %bitcast.328, f32[1024]{0:T(1024)S(1)} %bitcast.317, ...), kind=kOutput, calls=%fused_computation.107 | convolution fusion | flops 9747810304 | bytes 36783120 | tf_op jit(solution)/shard_map/isd,df->isf/dot_general | solution.py:131
  366.6 23.1 %convert_reduce_fusion = (f32[4096]{0:T(1024)}, bf16[2,577,4096]{2,1,0:T(8,128)(2,1)}) fusion(f32[2,577,4096]{2,1,0:T(8,128)} %get-tuple-element.112, f32[4096]{0:T(1024)S(1)} %bitcast.310, bf16[1,1024,4096]{2,1,0:T(8,128)(2,1)} %all-gather.11.cloned.1.call-done, f32[2]{0:T(128)S(1)} %fusion.133, bf16[1,2,1,577,1024]{4,1,3,2,0:T(2,128)(2,1)S(1)} %copy-done.21), kind=kOutput, calls=%fused_computation.24 | convolution fusion | flops 9745442816 | bytes 39145480 | tf_op jit(solution)/shard_map/isd,df->isf/dot_general | solution.py:140
  389.7 17.4 %fusion.144 = (f32[1024]{0:T(1024)}, f32[2,577]{1,0:T(2,128)S(1)}, f32[2,577,1024]{2,1,0:T(8,128)}) fusion(f32[1024]{0:T(1024)S(1)} %bitcast.318, f32[2,577,1024]{2,1,0:T(8,128)S(1)} %bitcast.293, f32[2,577]{1,0:T(2,128)S(1)} %broadcast_multiply_fusion, bf16[2,577,4096]{2,1,0:T(8,128)(2,1)} %get-tuple-element.122, ...), kind=kOutput, calls=%fused_computation.239 | convolution fusion | flops 9686360064 | bytes 27313168 | tf_op jit(solution)/shard_map/isf,df->isd/dot_general | solution.py:144
  431.0 19.4 %convert_reduce_fusion.2 = (f32[16,64]{1,0:T(8,128)}, bf16[2,16,64,577]{3,2,1,0:T(8,128)(2,1)}) fusion(bf16[2,577,16,64]{1,3,2,0:T(8,128)(2,1)S(1)} %bitcast.305, f32[2,16,577,577]{2,3,1,0:T(8,128)} %get-tuple-element.109, f32[2,16,577]{2,1,0:T(8,128)S(1)} %get-tuple-element.108), kind=kOutput, calls=%fused_computation.80 | convolution fusion | flops 1388528640 | bytes 47419648 | tf_op jit(solution)/shard_map/ihqk,iqhe->ikhe/dot_general | solution.py:154
  450.3 38.9 %multiply_reduce_fusion = (f32[2,16,577]{2,1,0:T(8,128)S(1)}, f32[2,16,577,577]{2,3,1,0:T(8,128)}) fusion(f32[2,16,577,577]{2,3,1,0:T(8,128)} %get-tuple-element.109, f32[2,16,577]{2,1,0:T(8,128)S(1)} %get-tuple-element.108, bf16[2,577,16,64]{1,3,2,0:T(8,128)(2,1)S(1)} %bitcast.306, f32[2,577,16,64]{1,3,2,0:T(8,128)} %bitcast.303, f32[16,64]{1,0:T(8,128)S(1)} %copy-done.61), kind=kOutput, calls=%fused_computation.2 | convolution fusion | flops 1397983232 | bytes 92471808 | tf_op jit(solution)/shard_map/iqhe,ikhe->ihqk/dot_general | solution.py:153
  489.3 39.1 %multiply_convert_fusion = bf16[2,16,577,577]{2,3,1,0:T(8,128)(2,1)} fusion(f32[2,16,577,577]{2,3,1,0:T(8,128)} %get-tuple-element.115, f32[2,16,577]{2,1,0:T(8,128)S(1)} %get-tuple-element.114, f32[2,16,577,577]{2,3,1,0:T(8,128)} %get-tuple-element.109, f32[2,16,577]{2,1,0:T(8,128)S(1)} %get-tuple-element.108), kind=kLoop, calls=%fused_computation.1 | loop fusion | flops 42614912 | bytes 106684992 | tf_op jit(solution)/shard_map/convert_element_type | solution.py:158
  580.8 19.6 %fusion.31 = bf16[1,1024,4096]{2,1,0:T(8,128)(2,1)} fusion(bf16[2,577,4096]{2,1,0:T(8,128)(2,1)} %get-tuple-element.122, f32[2,577,1024]{2,1,0:T(8,128)} %copy-done, f32[1024]{0:T(1024)S(1)} %bitcast.329, f32[1024]{0:T(1024)S(1)} %bitcast.321, f32[2,577]{1,0:T(2,128)S(1)} %copy-done.46, f32[2,577]{1,0:T(2,128)S(1)} %copy-done.34), kind=kOutput, calls=%fused_computation.58 | convolution fusion | flops 9690556416 | bytes 22586384 | tf_op jit(solution)/shard_map/isd,isf->df/dot_general | solution.py:142
  601.0 46.9 %fusion.7 = bf16[2,577,4096]{2,1,0:T(8,128)(2,1)S(1)} fusion(f32[2,577,4096]{2,1,0:T(8,128)} %get-tuple-element.112, f32[4096]{0:T(1024)S(1)} %bitcast.311, u8[577,4096]{1,0:T(8,128)(4,1)} %get-tuple-element.45, u8[577,4096]{1,0:T(8,128)(4,1)} %get-tuple-element.44), kind=kLoop, calls=%fused_computation.12 | loop fusion | flops 335601664 | bytes 33103872 | tf_op jit(solution)/shard_map/convert_element_type | solution.py:133
  713.7 16.4 %fusion.72 = bf16[1,2,1,577,1024]{4,3,1,2,0:T(8,128)(2,1)} fusion(f32[2,577,1024]{2,1,0:T(8,128)S(1)} %bitcast.295, f32[1024]{0:T(1024)S(1)} %bitcast.326, f32[2]{0:T(128)S(1)} %copy-done.70, bf16[2,577,4096]{2,1,0:T(8,128)(2,1)} %copy-done.16, bf16[1,1024,4096]{2,1,0:T(8,128)(2,1)} %all-gather.11.cloned.1.call-done), kind=kOutput, calls=%fused_computation.132 | convolution fusion | flops 9685180416 | bytes 24936456 | tf_op jit(solution)/shard_map/isf,df->isd/dot_general | solution.py:138
  731.1 42.1 %reduce-scatter.11.cloned.1.call-done = bf16[3,512,256]{1,2,0:T(8,128)(2,1)} async-done(((bf16[3,512,1024]{1,2,0:T(8,128)(2,1)}), bf16[3,512,256]{1,2,0:T(8,128)(2,1)}) %reduce-scatter.11.cloned.1.call-update) | async-done | bytes 786448 | tf_op jit(solution)/shard_map/reduce_scatter | solution.py:77
  781.5 70.9 %reduce-scatter.19.cloned.1.call-done = bf16[1,512,1024]{2,1,0:T(8,128)(2,1)} async-done(((bf16[1,512,4096]{2,1,0:T(8,128)(2,1)}), bf16[1,512,1024]{2,1,0:T(8,128)(2,1)}) %reduce-scatter.19.cloned.1.call-update) | async-done | bytes 1048592 | tf_op jit(solution)/shard_map/reduce_scatter | solution.py:77
  856.3 75.6 %reduce-scatter.23.cloned.1.call-done = bf16[1,512,1024]{2,1,0:T(8,128)(2,1)} async-done(((bf16[1,512,4096]{2,1,0:T(8,128)(2,1)}), bf16[1,512,1024]{2,1,0:T(8,128)(2,1)}) %reduce-scatter.23.cloned.1.call-update) | async-done | bytes 1048592 | tf_op jit(solution)/shard_map/reduce_scatter | solution.py:77
  969.5 28.7 %psum.30 = f32[12,1024]{1,0:T(8,128)S(1)} all-reduce(f32[12,1024]{1,0:T(8,128)S(1)} %concatenate.56), channel_id=1, replica_groups=mesh['group'=4,'fsdp'=2,'tensor'=4] {'fsdp','tensor'}, use_global_device_ids=true, to_apply=%region_30.31 | all-reduce | flops 12288 | bytes 98304 | tf_op jit(solution)/shard_map/psum | solution.py:194
  999.1 17.8 %psum.31 = f32[12,1024]{1,0:T(8,128)S(1)} all-reduce(f32[12,1024]{1,0:T(8,128)S(1)} %get-tuple-element.95), channel_id=1, replica_groups=mesh['group'=4,'fsdp'=2,'tensor'=4] {'group'}, use_global_device_ids=true, to_apply=%region_31.32 | all-reduce | flops 12288 | bytes 98304 | tf_op jit(solution)/shard_map/psum | solution.py:207
  (305 shorter events, 376.9 us)
Async XLA Ops:
  7.2 236.0 %all-gather.5.cloned.1.call-start = ((), (), s32[]{:S(2)}) async-start(), calls=%async_computation.8 | async-start | bytes 9437184 | tf_op jit(solution)/shard_map/all_gather | solution.py:71
  11.6 22.6 %collective-permute-start = (bf16[3,512,256]{2,1,0:T(8,128)(2,1)S(1)}, bf16[3,512,256]{2,1,0:T(8,128)(2,1)S(1)}, u32[]{:S(2)}, u32[]{:S(2)}) collective-permute-start(bf16[3,512,256]{2,1,0:T(8,128)(2,1)S(1)} %get-tuple-element.86), channel_id=1, source_target_pairs={{0,1},{1,2},{2,3},{3,0},{4,5},{5,6},{6,7},{7,4},{8,9},{9,10},{10,1... | collective-permute-start | bytes 2359304 | tf_op jit(solution)/shard_map/ppermute | solution.py:68
  35.1 20.6 %collective-permute-start.1 = (bf16[3,512,256]{2,1,0:T(8,128)(2,1)S(1)}, bf16[3,512,256]{2,1,0:T(8,128)(2,1)}, u32[]{:S(2)}, u32[]{:S(2)}) collective-permute-start(bf16[3,512,256]{2,1,0:T(8,128)(2,1)S(1)} %collective-permute-done), channel_id=1, source_target_pairs={{0,1},{1,2},{2,3},{3,0},{4,5},{5,6},{6,7},{7,4},{8,9},{9,10},{10,1... | collective-permute-start | bytes 2359304 | tf_op jit(solution)/shard_map/ppermute | solution.py:68
  55.7 19.9 %collective-permute-start.2 = (bf16[3,512,256]{2,1,0:T(8,128)(2,1)}, bf16[3,512,256]{2,1,0:T(8,128)(2,1)}, u32[]{:S(2)}, u32[]{:S(2)}) collective-permute-start(bf16[3,512,256]{2,1,0:T(8,128)(2,1)} %collective-permute-done.1), channel_id=1, source_target_pairs={{0,1},{1,2},{2,3},{3,0},{4,5},{5,6},{6,7},{7,4},{8,9},{9,10},{10,1... | collective-permute-start | bytes 2359304 | tf_op jit(solution)/shard_map/ppermute | solution.py:68
  78.6 251.0 %all-gather.7.cloned.1.call-start = ((), (), s32[]{:S(2)}) async-start(), calls=%async_computation.9 | async-start | bytes 3145728 | tf_op jit(solution)/shard_map/all_gather | solution.py:71
  85.5 38.2 %collective-permute-start.6 = (bf16[1,512,1024]{2,1,0:T(8,128)(2,1)S(1)}, bf16[1,512,1024]{2,1,0:T(8,128)(2,1)}, u32[]{:S(2)}, u32[]{:S(2)}) collective-permute-start(bf16[1,512,1024]{2,1,0:T(8,128)(2,1)S(1)} %get-tuple-element.78), channel_id=1, source_target_pairs={{0,1},{1,2},{2,3},{3,0},{4,5},{5,6},{6,7},{7,4},{8,9},{9,10},{10,1... | collective-permute-start | bytes 3145736 | tf_op jit(solution)/shard_map/ppermute | solution.py:68
  86.7 28.7 %collective-permute-start.3 = (bf16[1,512,256]{2,1,0:T(8,128)(2,1)S(1)}, bf16[1,512,256]{2,1,0:T(8,128)(2,1)S(1)}, u32[]{:S(2)}, u32[]{:S(2)}) collective-permute-start(bf16[1,512,256]{2,1,0:T(8,128)(2,1)S(1)} %get-tuple-element.84), channel_id=1, source_target_pairs={{0,1},{1,2},{2,3},{3,0},{4,5},{5,6},{6,7},{7,4},{8,9},{9,10},{10,1... | collective-permute-start | bytes 786440 | tf_op jit(solution)/shard_map/ppermute | solution.py:68
  123.7 11.0 %collective-permute-start.5 = (bf16[1,512,256]{2,1,0:T(8,128)(2,1)S(1)}, bf16[1,512,256]{2,1,0:T(8,128)(2,1)S(1)}, u32[]{:S(2)}, u32[]{:S(2)}) collective-permute-start(bf16[1,512,256]{2,1,0:T(8,128)(2,1)S(1)} %collective-permute-done.4), channel_id=1, source_target_pairs={{0,1},{1,2},{2,3},{3,0},{4,5},{5,6},{6,7},{7,4},{8,9},{9,10},{10,1... | collective-permute-start | bytes 786440 | tf_op jit(solution)/shard_map/ppermute | solution.py:68
  123.7 28.7 %collective-permute-start.7 = (bf16[1,512,1024]{2,1,0:T(8,128)(2,1)}, bf16[1,512,1024]{2,1,0:T(8,128)(2,1)}, u32[]{:S(2)}, u32[]{:S(2)}) collective-permute-start(bf16[1,512,1024]{2,1,0:T(8,128)(2,1)} %collective-permute-done.6), channel_id=1, source_target_pairs={{0,1},{1,2},{2,3},{3,0},{4,5},{5,6},{6,7},{7,4},{8,9},{9,10},{10,1... | collective-permute-start | bytes 3145736 | tf_op jit(solution)/shard_map/ppermute | solution.py:68
  135.8 202.9 %all-gather.9.cloned.1.call-start = ((), (), s32[]{:S(2)}) async-start(), calls=%async_computation.10 | async-start | bytes 12582912 | tf_op jit(solution)/shard_map/all_gather | solution.py:71
  152.4 22.2 %collective-permute-start.8 = (bf16[1,512,1024]{2,1,0:T(8,128)(2,1)}, bf16[1,512,1024]{2,1,0:T(8,128)(2,1)S(1)}, u32[]{:S(2)}, u32[]{:S(2)}) collective-permute-start(bf16[1,512,1024]{2,1,0:T(8,128)(2,1)} %collective-permute-done.7), channel_id=1, source_target_pairs={{0,1},{1,2},{2,3},{3,0},{4,5},{5,6},{6,7},{7,4},{8,9},{9,10},{10,1... | collective-permute-start | bytes 3145736 | tf_op jit(solution)/shard_map/ppermute | solution.py:68
  175.6 190.9 %all-gather.11.cloned.1.call-start = ((), (), s32[]{:S(2)}) async-start(), calls=%async_computation.11 | async-start | bytes 12582912 | tf_op jit(solution)/shard_map/all_gather | solution.py:71
  175.7 23.6 %collective-permute-start.9 = (bf16[1,512,1024]{2,1,0:T(8,128)(2,1)}, bf16[1,512,1024]{2,1,0:T(8,128)(2,1)S(1)}, u32[]{:S(2)}, u32[]{:S(2)}) collective-permute-start(bf16[1,512,1024]{2,1,0:T(8,128)(2,1)} %get-tuple-element.76), channel_id=1, source_target_pairs={{0,1},{1,2},{2,3},{3,0},{4,5},{5,6},{6,7},{7,4},{8,9},{9,10},{10,1... | collective-permute-start | bytes 3145736 | tf_op jit(solution)/shard_map/ppermute | solution.py:68
  199.3 23.1 %collective-permute-start.10 = (bf16[1,512,1024]{2,1,0:T(8,128)(2,1)S(1)}, bf16[1,512,1024]{2,1,0:T(8,128)(2,1)}, u32[]{:S(2)}, u32[]{:S(2)}) collective-permute-start(bf16[1,512,1024]{2,1,0:T(8,128)(2,1)S(1)} %collective-permute-done.9), channel_id=1, source_target_pairs={{0,1},{1,2},{2,3},{3,0},{4,5},{5,6},{6,7},{7,4},{8,9},{9,10},{10,1... | collective-permute-start | bytes 3145736 | tf_op jit(solution)/shard_map/ppermute | solution.py:68
  222.4 19.2 %collective-permute-start.11 = (bf16[1,512,1024]{2,1,0:T(8,128)(2,1)}, bf16[1,512,1024]{2,1,0:T(8,128)(2,1)S(1)}, u32[]{:S(2)}, u32[]{:S(2)}) collective-permute-start(bf16[1,512,1024]{2,1,0:T(8,128)(2,1)} %collective-permute-done.10), channel_id=1, source_target_pairs={{0,1},{1,2},{2,3},{3,0},{4,5},{5,6},{6,7},{7,4},{8,9},{9,10},{10,1... | collective-permute-start | bytes 3145736 | tf_op jit(solution)/shard_map/ppermute | solution.py:68
  242.6 424.3 %reduce-scatter.13.cloned.1.call-start = ((), (), s32[]{:S(2)}) async-start(), calls=%async_computation.14 | async-start | bytes 3145728 | tf_op jit(solution)/shard_map/reduce_scatter | solution.py:76
  489.2 178.4 %reduce-scatter.9.cloned.1.call-start = ((), (), s32[]{:S(2)}) async-start(), calls=%async_computation.12 | async-start | bytes 9437184 | tf_op jit(solution)/shard_map/reduce_scatter | solution.py:76
  580.1 88.1 %reduce-scatter.17.cloned.1.call-start = ((), (), s32[]{:S(2)}) async-start(), calls=%async_computation.16 | async-start | bytes 12582912 | tf_op jit(solution)/shard_map/reduce_scatter | solution.py:76
  600.4 80.9 %reduce-scatter.21.cloned.1.call-start = ((), (), s32[]{:S(2)}) async-start(), calls=%async_computation.18 | async-start | bytes 12582912 | tf_op jit(solution)/shard_map/reduce_scatter | solution.py:76
  666.8 63.2 %reduce-scatter.15.cloned.1.call-start = ((), (), s32[]{:S(2)}) async-start(), calls=%async_computation.15 | async-start | bytes 1310720 | tf_op jit(solution)/shard_map/reduce_scatter | solution.py:77
  667.6 105.7 %reduce-scatter.11.cloned.1.call-start = ((), (), s32[]{:S(2)}) async-start(), calls=%async_computation.13 | async-start | bytes 3932160 | tf_op jit(solution)/shard_map/reduce_scatter | solution.py:77
  668.1 184.3 %reduce-scatter.19.cloned.1.call-start = ((), (), s32[]{:S(2)}) async-start(), calls=%async_computation.17 | async-start | bytes 5242880 | tf_op jit(solution)/shard_map/reduce_scatter | solution.py:77
  668.9 263.0 %reduce-scatter.23.cloned.1.call-start = ((), (), s32[]{:S(2)}) async-start(), calls=%async_computation.19 | async-start | bytes 5242880 | tf_op jit(solution)/shard_map/reduce_scatter | solution.py:77
  681.3 355.3 %all-reduce.3.cloned.1.call-start = ((), (), s32[]{:S(2)}) async-start(), calls=%async_computation.20 | async-start | bytes 6291456 | tf_op jit(solution)/shard_map/psum | solution.py:204
  (79 other events, 2389.9 us)
Sparse Core Ops, SparseCore 0:
  78.7 14.4 all-gather.4
  135.9 8.2 all-gather.6
  175.8 17.5 all-gather.8
  242.7 17.3 all-gather.10
  489.3 7.9 reduce-scatter.12
  580.2 12.9 reduce-scatter.8
  600.5 14.2 reduce-scatter.16
  666.9 14.3 reduce-scatter.20
  683.6 28.3 reduce-scatter.14
  714.3 58.8 reduce-scatter.10
  775.6 76.7 reduce-scatter.18
  854.6 77.2 reduce-scatter.22
  943.0 88.6 all-reduce.2
